TPU v7x, 32 devices: a 4x2x2 block of a 4x4x8 slice. The times are simulated.
32 devices in a mesh: dp: 4 (over y, z), tp: 8 (over x, core).
Axes of the slice: x: 4, y: 2, z: 2, core: 2. Of those that a mesh axis runs over, the one named last changes fastest.
The devices are a block of a 4x4x8 slice.
Arguments:
- x: bfloat16 [16, 1536, 3584], P('dp'), parts along dimension 0
- gamma: float32 [3584], replicated
- beta: float32 [3584], replicated
- wq: bfloat16 [3584, 4096], P(None, 'tp')
- wkv: bfloat16 [3584, 512], replicated
- wo: bfloat16 [4096, 3584], P('tp')
- w1: bfloat16 [3584, 14336], P(None, 'tp')
- w3: bfloat16 [3584, 14336], P(None, 'tp')
- w2: bfloat16 [14336, 3584], P('tp')
Outputs:
- output: bfloat16 [16, 1536, 3584], P('dp'), parts along dimension 0
There are 4 independent parts. A program takes and returns all parts, laid end to end along the dimension named above; an argument that names none is the same for every part.
All inputs are finite; a program needn't handle non-finite values.
Results may differ from a plain program's by a relative error of at most 0.0125769.
Values are sent between devices in bfloat16 or wider.
A program may use at most 768 MiB of HBM per device.

v0:
```python
import jax
import jax.numpy as jnp
from jax import lax
from jax.sharding import PartitionSpec as P

EPS = 1e-5


def solution(mesh):
    def local(x, gamma, beta, wq, wkv, wo, w1, w3, w2):
        b, s, d = x.shape
        dh = wkv.shape[1] // 2
        nh = wq.shape[1] // dh
        xf = x.astype(jnp.float32)
        mu = jnp.mean(xf, axis=-1, keepdims=True)
        var = jnp.mean(jnp.square(xf - mu), axis=-1, keepdims=True)
        ln = ((xf - mu) * lax.rsqrt(var + EPS) * gamma + beta).astype(jnp.bfloat16).reshape(b * s, d)
        q = jnp.dot(ln, wq, preferred_element_type=jnp.float32).astype(jnp.bfloat16).reshape(b, s, nh, dh)
        kv = jnp.dot(ln, wkv, preferred_element_type=jnp.float32).astype(jnp.bfloat16).reshape(b, s, 2 * dh)
        k = kv[:, :, :dh]
        v = kv[:, :, dh:]
        sc = jnp.einsum('bqhe,bke->bhqk', q, k, preferred_element_type=jnp.float32) * dh ** -0.5
        qi = lax.broadcasted_iota(jnp.int32, (s, s), 0)
        ki = lax.broadcasted_iota(jnp.int32, (s, s), 1)
        sc = jnp.where(ki <= qi, sc, -1e30)
        p = jax.nn.softmax(sc, axis=-1).astype(jnp.bfloat16)
        o = jnp.einsum('bhqk,bke->bqhe', p, v, preferred_element_type=jnp.float32).astype(jnp.bfloat16).reshape(b * s, nh * dh)
        a = jnp.dot(o, wo, preferred_element_type=jnp.float32)
        g = jnp.dot(ln, w1, preferred_element_type=jnp.float32)
        u = jnp.dot(ln, w3, preferred_element_type=jnp.float32)
        hm = (jax.nn.silu(g) * u).astype(jnp.bfloat16)
        m = jnp.dot(hm, w2, preferred_element_type=jnp.float32)
        part = (a + m).astype(jnp.bfloat16)
        tot = lax.psum(part, 'tp')
        return (xf + tot.astype(jnp.float32).reshape(b, s, d)).astype(jnp.bfloat16)

    return jax.shard_map(local, mesh=mesh,
                         in_specs=(P('dp', None, None), P(), P(), P(None, 'tp'), P(), P('tp', None),
                                   P(None, 'tp'), P(None, 'tp'), P('tp', None)),
                         out_specs=P('dp', None, None), check_vma=False)
```

profile of v0, /device:TPU:81, one launch (start us, length us, event | category | flops | bytes accessed | tf_op | source)
XLA Modules:
  0.0 1033.7 jit_solution(17810487314435792292)
XLA Ops:
  6.5 0.0 all-reduce.2.cloned.1.call-start
  6.6 2.1 iota_compare_fusion
  8.6 0.0 copy-start.1
  8.6 0.0 copy-start.2
  8.6 14.6 %convert_reduce_fusion = f32[4,1536]{1,0:T(4,128)S(1)} fusion(bf16[4,1536,3584]{2,1,0:T(8,128)(2,1)} %param.9), kind=kLoop, calls=%fused_computation.3 | loop fusion | flops 44034048 | bytes 44064768 | tf_op jit(solution)/shard_map/reduce_sum | solution.py:15
  23.3 19.5 %fusion.3 = f32[4,1536]{1,0:T(4,128)S(1)} fusion(bf16[4,1536,3584]{2,1,0:T(8,128)(2,1)} %param.9, f32[4,1536]{1,0:T(4,128)S(1)} %broadcast_multiply_fusion), kind=kLoop, calls=%fused_computation.6 | loop fusion | flops 88074240 | bytes 44089344 | tf_op jit(solution)/shard_map/reduce_sum | solution.py:16
  42.8 0.0 copy-done.1
  42.8 0.0 copy-done.2
  42.9 0.0 copy-start.3
  42.9 29.8 %fusion.6 = bf16[4,1536,3584]{2,1,0:T(8,128)(2,1)} fusion(bf16[4,1536,3584]{2,1,0:T(8,128)(2,1)} %param.9, f32[3584]{0:T(1024)S(1)} %copy-done.1, f32[3584]{0:T(1024)S(1)} %copy-done.2, f32[4,1536]{1,0:T(4,128)S(1)} %add_rsqrt_fusion, f32[4,1536]{1,0:T(4,128)S(1)} %broadcast_multiply_fusion), kind=kLoop, calls=%fused_computation.9 | loop fusion | flops 132120576 | bytes 88158208 | tf_op jit(solution)/shard_map/convert_element_type | solution.py:17
  72.7 0.6 copy-done.3
  73.3 30.1 %convolution_convert_fusion = bf16[6144,512]{1,0:T(8,128)(2,1)} fusion(bf16[6144,3584]{1,0:T(8,128)(2,1)} %bitcast.42, bf16[3584,512]{1,0:T(8,128)(2,1)S(1)} %copy-done.3), kind=kOutput, calls=%fused_computation.22 | convolution fusion | flops 22551724032 | bytes 54001664 | tf_op jit(solution)/shard_map/dot_general | solution.py:18
  103.3 9.7 reshape.36
  113.1 31.5 %convolution_convert_fusion.1 = bf16[6144,512]{1,0:T(8,128)(2,1)} fusion(bf16[6144,3584]{1,0:T(8,128)(2,1)} %bitcast.43, bf16[3584,512]{1,0:T(8,128)(2,1)} %param.13), kind=kOutput, calls=%fused_computation.23 | convolution fusion | flops 22551724032 | bytes 54001664 | tf_op jit(solution)/shard_map/dot_general | solution.py:19
  144.5 0.0 copy-start
  144.5 90.4 %fusion.27 = f32[6144,1792]{1,0:T(8,128)} fusion(bf16[6144,3584]{1,0:T(8,128)(2,1)} %bitcast.44, bf16[3584,1792]{1,0:T(8,128)(2,1)} %param.15), kind=kOutput, calls=%fused_computation.37 | convolution fusion | flops 78920024064 | bytes 100925440 | tf_op jit(solution)/shard_map/dot_general | solution.py:29
  234.9 0.0 copy-done
  234.9 36.6 %fusion.23 = (f32[4,2,1536]{2,1,0:T(2,128)S(1)}, f32[4,2,1536,1536]{2,3,1,0:T(8,128)}) fusion(pred[1536,1536]{0,1:T(8,128)(4,1)S(1)} %copy-done, bf16[4,1536,2,256]{3,2,1,0:T(2,128)(2,1)} %reshape.36, bf16[4,1536,512]{2,1,0:T(8,128)(2,1)} %bitcast.48), kind=kOutput, calls=%fused_computation.35 | convolution fusion | flops 9739174912 | bytes 87343104 | tf_op jit(solution)/shard_map/sub | solution.py:26
  271.5 29.2 %convert_bitcast_fusion = bf16[4,1536,2,256]{1,3,2,0:T(8,128)(2,1)} fusion(f32[4,2,1536,1536]{2,3,1,0:T(8,128)} %get-tuple-element.6, f32[4,2,1536]{2,1,0:T(2,128)S(1)} %get-tuple-element.5, bf16[4,1536,512]{2,1,0:T(8,128)(2,1)} %bitcast.49), kind=kOutput, calls=%fused_computation.25 | convolution fusion | flops 9704570880 | bytes 84983808 | tf_op jit(solution)/shard_map/bhqk,bke->bqhe/dot_general | solution.py:27
  300.7 16.1 %copy.16 = bf16[4,1536,2,256]{3,2,1,0:T(2,128)(2,1)} copy(bf16[4,1536,2,256]{1,3,2,0:T(8,128)(2,1)} %convert_bitcast_fusion) | data formatting | bytes 12582912 | tf_op jit(solution)/shard_map/convert_element_type | solution.py:27
  316.8 6.5 copy.22
  323.3 0.0 copy-start.4
  323.3 92.1 %multiply_convert_fusion = bf16[6144,1792]{1,0:T(8,128)(2,1)} fusion(f32[6144,1792]{1,0:T(8,128)} %fusion.27, bf16[6144,3584]{1,0:T(8,128)(2,1)} %bitcast.45, bf16[3584,1792]{1,0:T(8,128)(2,1)} %param.16), kind=kOutput, calls=%fused_computation.16 | convolution fusion | flops 78986084352 | bytes 122945536 | tf_op jit(solution)/shard_map/dot_general | solution.py:30
  415.4 0.0 copy-done.4
  415.4 37.9 %fusion.26 = f32[6144,3584]{1,0:T(8,128)} fusion(bf16[6144,512]{1,0:T(8,128)(2,1)} %bitcast.47, bf16[512,3584]{1,0:T(8,128)(2,1)S(1)} %copy-done.4), kind=kOutput, calls=%fused_computation.36 | convolution fusion | flops 22548578304 | bytes 98041856 | tf_op jit(solution)/shard_map/dot_general | solution.py:28
  453.3 92.4 %add_convert_fusion = bf16[6144,3584]{1,0:T(8,128)(2,1)} fusion(f32[6144,3584]{1,0:T(8,128)} %fusion.26, bf16[6144,1792]{1,0:T(8,128)(2,1)} %multiply_convert_fusion, bf16[1792,3584]{1,0:T(8,128)(2,1)} %param.17), kind=kOutput, calls=%fused_computation.11 | convolution fusion | flops 78964064256 | bytes 166985728 | tf_op jit(solution)/shard_map/dot_general | solution.py:32
  545.8 0.1 all-reduce.2.cloned.1.call-update
  545.8 436.7 %all-reduce.2.cloned.1.call-done = bf16[4,1536,3584]{2,1,0:T(8,128)(2,1)} async-done(((bf16[4,1536,3584]{2,1,0:T(8,128)(2,1)}), bf16[4,1536,3584]{2,1,0:T(8,128)(2,1)}) %all-reduce.2.cloned.1.call-update) | async-done | bytes 44040208 | tf_op jit(solution)/shard_map/psum | solution.py:34
  982.5 43.8 %fusion.7 = bf16[4,1536,3584]{2,1,0:T(8,128)(2,1)} fusion(bf16[4,1536,3584]{2,1,0:T(8,128)(2,1)} %param.9, bf16[4,1536,3584]{2,1,0:T(8,128)(2,1)} %all-reduce.2.cloned.1.call-done), kind=kLoop, calls=%fused_computation.10 | loop fusion | flops 88080384 | bytes 132120576 | tf_op jit(solution)/shard_map/convert_element_type | solution.py:35
  (2 shorter events, 0.0 us)
Async XLA Ops:
  6.5 975.9 %all-reduce.2.cloned.1.call-start = ((), (), s32[]{:S(2)}) async-start(), calls=%async_computation | async-start | bytes 88080384 | tf_op jit(solution)/shard_map/psum | solution.py:34
  8.6 34.2 %copy-start.1 = (f32[3584]{0:T(1024)S(1)}, f32[3584]{0:T(1024)}, u32[]{:S(2)}) copy-start(f32[3584]{0:T(1024)} %param.11) | copy-start | bytes 43012
  8.6 34.2 %copy-start.2 = (f32[3584]{0:T(1024)S(1)}, f32[3584]{0:T(1024)}, u32[]{:S(2)}) copy-start(f32[3584]{0:T(1024)} %param.10) | copy-start | bytes 43012
  42.9 30.4 %copy-start.3 = (bf16[3584,512]{1,0:T(8,128)(2,1)S(1)}, bf16[3584,512]{1,0:T(8,128)(2,1)}, u32[]{:S(2)}) copy-start(bf16[3584,512]{1,0:T(8,128)(2,1)} %param.12) | copy-start | bytes 11010052
  144.5 90.4 %copy-start = (pred[1536,1536]{0,1:T(8,128)(4,1)S(1)}, pred[1536,1536]{0,1:T(8,128)(4,1)}, u32[]{:S(2)}) copy-start(pred[1536,1536]{0,1:T(8,128)(4,1)} %iota_compare_fusion) | copy-start | bytes 7077892
  323.3 92.1 %copy-start.4 = (bf16[512,3584]{1,0:T(8,128)(2,1)S(1)}, bf16[512,3584]{1,0:T(8,128)(2,1)}, u32[]{:S(2)}) copy-start(bf16[512,3584]{1,0:T(8,128)(2,1)} %param.14) | copy-start | bytes 11010052
Sparse Core Ops, SparseCore 0:
  545.9 436.4 all-reduce.1
where the time goes:
time: 1040 us; the launch traced here: 1030 us
  matrix products  440 us (42%)
  waiting for transfers between devices  437 us (42%)
  other arithmetic  110 us (11%)
  local copies, waits for them, and re-layouts  32.9 us (3%)
  between operations  14 us (1%)
    psum x1, waiting for transfers between devices, local(): tot = lax.psum(part, 'tp')  437 us
    dot_general x1, matrix products, local(): m = jnp.dot(hm, w2, preferred_element_type=jnp.float32)  92.4 us
    dot_general x1, matrix products, local(): u = jnp.dot(ln, w3, preferred_element_type=jnp.float32)  92.1 us
    dot_general x1, matrix products, local(): g = jnp.dot(ln, w1, preferred_element_type=jnp.float32)  90.4 us
    convert_element_type x1, other arithmetic, local(): return (xf + tot.astype(jnp.float32).reshape(b, s, d)).astype(jnp.bfloat16)  43.8 us
    dot_general x1, matrix products, local(): a = jnp.dot(o, wo, preferred_element_type=jnp.float32)  37.9 us
    sub x1, matrix products, local(): p = jax.nn.softmax(sc, axis=-1).astype(jnp.bfloat16)  36.6 us
    dot_general x1, matrix products, local(): jnp.dot(ln, wkv, preferred_element_type=jnp.float32).astype(jnp.bfloat16)  31.5 us
  transfers between devices with their start and end apart: 1, of which 1 were waited for; matrix products, arithmetic and copies ran while one was open for 0% of the time, Pallas kernels for 0%

commit v1 on v0

v1 whole, which is shorter than its diff:
```python
import functools

import jax
import jax.numpy as jnp
from jax import lax
from jax.experimental import pallas as pl
from jax.experimental.pallas import tpu as pltpu
from jax.sharding import PartitionSpec as P

EPS = 1e-5
MESH = pl.DeviceIdType.MESH
TOK = 256
LOG2E = 1.4426950408889634
F32 = jnp.float32
BF16 = jnp.bfloat16


def kernel(n_tp, seq,
           x, gamma, beta, wq, wkv, wo, w1, w3, w2,
           y,
           wqkv, w13, w2o, xin, lnst, ln, kv, act, part, pbuf, r1, r2, ybuf, xres,
           wsem, xsem, xrsem, lns, lnr, lnfree, kvs, kvr, ds_, dr_, s1s, s1r, s2s, s2r,
           ys, yr, fs, fr, gs, gr):
    d = x.shape[1]
    n = x.shape[0] // TOK
    per_seq = seq // TOK
    dq = wq.shape[1]
    dh = wkv.shape[1] // 2
    ff = w1.shape[1]
    nh = dq // dh
    half = TOK // 2
    chips = n_tp // 2
    blk = half // chips
    dm = d // 2

    me = lax.axis_index("tp")
    h = lax.rem(me, 2)
    c = me // 2
    cp = lax.rem(c + 1, chips)
    cm = lax.rem(c + chips - 1, chips)
    co = lax.rem(c + 2, chips)
    plus, minus, partner = cp * 2 + h, cm * 2 + h, c * 2 + 1 - h

    def rcopy(src, dst, ssem, rsem, dev):
        return pltpu.make_async_remote_copy(src_ref=src, dst_ref=dst, send_sem=ssem, recv_sem=rsem,
                                            device_id={"tp": dev}, device_id_type=MESH)

    def own(ref):
        return ref.at[pl.ds(pl.multiple_of(h * half, half), half)]

    def other(ref):
        return ref.at[pl.ds(pl.multiple_of((1 - h) * half, half), half)]

    def rows_of(k):
        return pl.ds(pl.multiple_of(k * blk, blk), blk)

    def yrows(j, k):
        return pl.ds(pl.multiple_of(j * TOK + h * half + k * blk, blk), blk)

    def x_copy(j):
        return pltpu.make_async_copy(x.at[pl.ds(pl.multiple_of(j * TOK + h * half, half), half)], xin, xsem)

    def xres_copy(j):
        return pltpu.make_async_copy(x.at[yrows(j, c)], xres.at[lax.rem(j, 2)], xrsem.at[lax.rem(j, 2)])

    w_copies = (
        pltpu.make_async_copy(wq, wqkv.at[:, pl.ds(0, dq)], wsem.at[0]),
        pltpu.make_async_copy(wkv.at[:, pl.ds(pl.multiple_of(h * dh, dh), dh)], wqkv.at[:, pl.ds(dq, dh)], wsem.at[1]),
        pltpu.make_async_copy(w1, w13.at[:, pl.ds(0, ff)], wsem.at[2]),
        pltpu.make_async_copy(w3, w13.at[:, pl.ds(ff, ff)], wsem.at[3]),
        pltpu.make_async_copy(wo, w2o.at[pl.ds(0, dq)], wsem.at[4]),
        pltpu.make_async_copy(w2, w2o.at[pl.ds(dq, ff)], wsem.at[5]),
    )

    def layer_norm():
        for r in range(0, half, 16):
            xf = xin[r:r + 16, :].astype(F32)
            mu = jnp.mean(xf, axis=-1, keepdims=True)
            xc = xf - mu
            var = jnp.mean(jnp.square(xc), axis=-1, keepdims=True)
            lnst[r:r + 16, :] = (xc * lax.rsqrt(var + EPS) * gamma[...] + beta[...]).astype(BF16)

    def ln_local():
        ln[pl.ds(pl.multiple_of(h * half, half), half), :] = lnst[...]

    def ln_copy():
        return rcopy(lnst, own(ln), lns, lnr, partner)

    def kv_copy(t):
        view = kv.at[h, pl.ds(pl.multiple_of(lax.rem(t, per_seq) * TOK, TOK), TOK)]
        return rcopy(view, view, kvs, kvr, partner)

    def d2d_copy(j):
        s = lax.rem(j, 2)
        return rcopy(other(part), pbuf.at[s], ds_.at[s], dr_.at[s], partner)

    def s1_copies(j):
        s = lax.rem(j, 2)
        return (rcopy(pbuf.at[s, rows_of(co), pl.ds(0, dm)], r1.at[s, 0], s1s.at[s, 0], s1r.at[s, 0], plus),
                rcopy(pbuf.at[s, rows_of(co), pl.ds(dm, dm)], r1.at[s, 1], s1s.at[s, 1], s1r.at[s, 1], minus))

    def s2_copies(j):
        s = lax.rem(j, 2)
        return (rcopy(pbuf.at[s, rows_of(cp)], r2.at[s, 0], s2s.at[s, 0], s2r.at[s, 0], plus),
                rcopy(pbuf.at[s, rows_of(cm)], r2.at[s, 1], s2s.at[s, 1], s2r.at[s, 1], minus))

    def y_copies(j, ks):
        s, s3 = lax.rem(j, 2), lax.rem(j, 3)
        return tuple(rcopy(ybuf.at[s], y.at[yrows(j, k)], ys.at[s3, i], yr.at[s3, i], dev)
                     for i, (k, dev) in enumerate(zip(ks, (plus, minus, partner))))

    def y_local(j):
        return pltpu.make_async_copy(ybuf.at[lax.rem(j, 2)], y.at[yrows(j, c)], ys.at[lax.rem(j, 3), 3])

    def f_copies(j):
        s3 = lax.rem(j, 3)
        va = y.at[yrows(j, cm), pl.ds(0, dm)]
        vb = y.at[yrows(j, cp), pl.ds(dm, dm)]
        vm, vp = y.at[yrows(j, cm)], y.at[yrows(j, cp)]
        return (rcopy(va, va, fs.at[s3, 0], fr.at[s3, 0], plus),
                rcopy(vb, vb, fs.at[s3, 1], fr.at[s3, 1], minus),
                rcopy(vm, vm, fs.at[s3, 2], fr.at[s3, 2], partner),
                rcopy(vp, vp, fs.at[s3, 3], fr.at[s3, 3], partner))

    def g_copy(j):
        s3 = lax.rem(j, 3)
        v = y.at[yrows(j, co)]
        return rcopy(v, v, gs.at[s3], gr.at[s3], partner)

    def s1(j):
        s = lax.rem(j, 2)
        cpy = d2d_copy(j)
        cpy.wait_recv()
        cpy.wait_send()

        @pl.loop(0, half // 32)
        def _(i):
            a = part[pl.ds(pl.multiple_of(h * half + i * 32, 32), 32), :].astype(F32)
            rr = pl.ds(pl.multiple_of(i * 32, 32), 32)
            pbuf[s, rr, :] = (a + pbuf[s, rr, :].astype(F32)).astype(BF16)

        for cpy in s1_copies(j):
            cpy.start()
        xres_copy(j).start()

    def s2(j):
        s = lax.rem(j, 2)
        first = s1_copies(j)
        for cpy in first:
            cpy.wait_recv()
        pbuf[s, rows_of(cp), :dm] = (pbuf[s, rows_of(cp), :dm].astype(F32) + r1[s, 0].astype(F32)).astype(BF16)
        pbuf[s, rows_of(cm), dm:] = (pbuf[s, rows_of(cm), dm:].astype(F32) + r1[s, 1].astype(F32)).astype(BF16)
        for cpy in s2_copies(j):
            cpy.start()
        for cpy in first:
            cpy.wait_send()

    def s3(j):
        s = lax.rem(j, 2)
        second = s2_copies(j)
        for cpy in second:
            cpy.wait_recv()
        xres_copy(j).wait()
        ybuf[s] = (xres[s].astype(F32) + ((pbuf[s, rows_of(c), :].astype(F32) + r2[s, 0].astype(F32))
                                          + r2[s, 1].astype(F32))).astype(BF16)
        for cpy in y_copies(j, (c, c, c)):
            cpy.start()
        y_local(j).start()
        for cpy in second:
            cpy.wait_send()

    def s4(j):
        for cpy in y_copies(j, (cm, cp, c)):
            cpy.wait_recv()
        for cpy in f_copies(j):
            cpy.start()
        for cpy in y_copies(j, (c, c, c)):
            cpy.wait_send()
        y_local(j).wait()

    def s5(j):
        for cpy in f_copies(j):
            cpy.wait_recv()
        g_copy(j).start()
        for cpy in f_copies(j):
            cpy.wait_send()

    def s6(j):
        g_copy(j).wait_recv()
        g_copy(j).wait_send()

    def attention(blocks):
        keys = blocks * TOK
        k = kv[0, :keys, :]
        v = kv[1, :keys, :]
        qi = lax.broadcasted_iota(jnp.int32, (TOK, TOK), 0)
        ki = lax.broadcasted_iota(jnp.int32, (TOK, TOK), 1)
        for a in range(nh):
            q = act[:, a * dh:(a + 1) * dh]
            sc = lax.dot_general(q, k, (((1,), (1,)), ((), ())), preferred_element_type=F32)
            sc = sc * (dh ** -0.5 * LOG2E)
            last = jnp.where(ki <= qi, sc[:, keys - TOK:], -1e30)
            sc = last if blocks == 1 else jnp.concatenate([sc[:, :keys - TOK], last], axis=1)
            p = jnp.exp2(sc - jnp.max(sc, axis=-1, keepdims=True))
            p = (p * (1.0 / jnp.sum(p, axis=-1, keepdims=True))).astype(BF16)
            act[:, a * dh:(a + 1) * dh] = jnp.dot(p, v, preferred_element_type=F32).astype(BF16)

    barrier = pltpu.get_barrier_semaphore()
    for dev in (partner, plus, minus):
        pl.semaphore_signal(barrier, inc=1, device_id={"tp": dev}, device_id_type=MESH)
    x_copy(0).start()
    for cpy in w_copies:
        cpy.start()
    pl.semaphore_wait(barrier, 3)
    x_copy(0).wait()
    layer_norm()
    ln_local()
    x_copy(1).start()
    ln_copy().start()

    @pl.loop(0, n + 5)
    def _(t):
        @pl.when(t < n)
        def _():
            ln_copy().wait_recv()
            ln_copy().wait_send()

            @pl.when(t == 0)
            def _():
                w_copies[0].wait()
                w_copies[1].wait()

            @pl.when(t + 1 < n)
            def _():
                x_copy(t + 1).wait()

            layer_norm()
            pos = pl.multiple_of(lax.rem(t, per_seq) * TOK, TOK)
            qkv = jnp.dot(ln[...], wqkv[...], preferred_element_type=F32).astype(BF16)
            act[:, :dq] = qkv[:, :dq]
            kv[h, pl.ds(pos, TOK), :] = qkv[:, dq:]

            @pl.when(t + 2 < n)
            def _():
                x_copy(t + 2).start()

        @pl.when((t >= 1) & (t <= n))
        def _():
            s1(t - 1)

        @pl.when((t >= 2) & (t <= n + 1))
        def _():
            s3(t - 2)

        @pl.when(t < n)
        def _():
            kv_copy(t).start()

            @pl.when(t == 0)
            def _():
                w_copies[2].wait()
                w_copies[3].wait()

            lhs = ln[...]
            tile = min(256, ff)
            for j in range(0, ff, tile):
                g = jnp.dot(lhs, w13[:, j:j + tile], preferred_element_type=F32)
                u = jnp.dot(lhs, w13[:, ff + j:ff + j + tile], preferred_element_type=F32)
                act[:, dq + j:dq + j + tile] = (jax.nn.silu(g) * u).astype(BF16)

            @pl.when(t + 1 < n)
            def _():
                pl.semaphore_signal(lnfree, inc=1, device_id={"tp": partner}, device_id_type=MESH)
                ln_local()

        @pl.when((t >= 1) & (t <= n))
        def _():
            s2(t - 1)

        @pl.when((t >= 3) & (t <= n + 2))
        def _():
            s4(t - 3)

        @pl.when((t >= 4) & (t <= n + 3))
        def _():
            s5(t - 4)

        @pl.when(t >= 5)
        def _():
            s6(t - 5)

        @pl.when(t < n)
        def _():
            kv_copy(t).wait_recv()
            kv_copy(t).wait_send()
            for b in range(per_seq):
                pl.when(lax.rem(t, per_seq) == b)(functools.partial(attention, b + 1))

            @pl.when(t + 1 < n)
            def _():
                pl.semaphore_wait(lnfree, 1)
                ln_copy().start()

            @pl.when(t == 0)
            def _():
                w_copies[4].wait()
                w_copies[5].wait()

            lhs = act[...]
            tile = min(512, d)
            for j in range(0, d, tile):
                part[:, j:j + tile] = jnp.dot(lhs, w2o[:, j:j + tile], preferred_element_type=F32).astype(BF16)
            d2d_copy(t).start()


def solution(mesh):
    n_tp = mesh.shape["tp"]

    def local(x, gamma, beta, wq, wkv, wo, w1, w3, w2):
        b, s, d = x.shape
        dq, dh, ff = wq.shape[1], wkv.shape[1] // 2, w1.shape[1]
        half = TOK // 2
        blk = half // (n_tp // 2)
        dma = pltpu.SemaphoreType.DMA
        hbm = pl.BlockSpec(memory_space=pl.ANY)
        vmem = pl.BlockSpec(memory_space=pltpu.VMEM)
        out = pl.pallas_call(
            functools.partial(kernel, n_tp, s),
            out_shape=jax.ShapeDtypeStruct((b * s, d), BF16),
            in_specs=[hbm, vmem, vmem] + [hbm] * 6,
            out_specs=hbm,
            scratch_shapes=[
                pltpu.VMEM((d, dq + dh), BF16),
                pltpu.VMEM((d, 2 * ff), BF16),
                pltpu.VMEM((dq + ff, d), BF16),
                pltpu.VMEM((half, d), BF16),
                pltpu.VMEM((half, d), BF16),
                pltpu.VMEM((TOK, d), BF16),
                pltpu.VMEM((2, s, dh), BF16),
                pltpu.VMEM((TOK, dq + ff), BF16),
                pltpu.VMEM((TOK, d), BF16),
                pltpu.VMEM((2, half, d), BF16),
                pltpu.VMEM((2, 2, blk, d // 2), BF16),
                pltpu.VMEM((2, 2, blk, d), BF16),
                pltpu.VMEM((2, blk, d), BF16),
                pltpu.VMEM((2, blk, d), BF16),
                dma((6,)), dma, dma((2,)), dma, dma, pltpu.SemaphoreType.REGULAR, dma, dma,
                dma((2,)), dma((2,)), dma((2, 2)), dma((2, 2)), dma((2, 2)), dma((2, 2)),
                dma((3, 4)), dma((3, 3)), dma((3, 4)), dma((3, 4)), dma((3,)), dma((3,)),
            ],
            compiler_params=pltpu.CompilerParams(collective_id=0, has_side_effects=True,
                                                 vmem_limit_bytes=67043328),
        )(x.reshape(b * s, d), gamma.reshape(1, d), beta.reshape(1, d), wq, wkv, wo, w1, w3, w2)
        return out.reshape(b, s, d)

    return jax.shard_map(local, mesh=mesh,
                         in_specs=(P('dp', None, None), P(), P(), P(None, 'tp'), P(), P('tp', None),
                                   P(None, 'tp'), P(None, 'tp'), P('tp', None)),
                         out_specs=P('dp', None, None), check_vma=False)
```

time: 1040 us -> 458 us (0.44)
  matrix products: 440 us -> 0 us
  waiting for transfers between devices: 437 us -> 0 us
  Pallas kernels: 0 us -> 426 us
  other arithmetic: 110 us -> 0 us
  between operations: 14 us -> 0.01 us
    psum x1 -> x0, waiting for transfers between devices: 437 us -> none  [local(): tot = lax.psum(part, 'tp')]
    pallas_call x0 -> x1, Pallas kernels: none -> 426 us  [local(): pl.pallas_call(functools.partial(kernel, n_tp, s), out_shape=jax.ShapeDty...]
    dot_general x7 -> x0, matrix products: 404 us -> none  [the longest x1 92.4 us: local(): m = jnp.dot(hm, w2, preferred_element_type=jnp.float32)]
    convert_element_type x2 -> x0, other arithmetic: 73.6 us -> none  [the longest x1 43.8 us: local(): return (xf + tot.astype(jnp.float32).reshape(b, s, d)).astype(jnp.bfloat16)]
    sub x1 -> x0, matrix products: 36.6 us -> none  [local(): p = jax.nn.softmax(sc, axis=-1).astype(jnp.bfloat16)]
    reduce_sum x2 -> x0, other arithmetic: 34.1 us -> none  [the longest x1 19.5 us: local(): var = jnp.mean(jnp.square(xf - mu), axis=-1, keepdims=True)]
    unnamed x11 -> x1, local copies, waits for them, and re-layouts: 7.15 us -> 29 us
    convert_element_type x1 -> x0, local copies, waits for them, and re-layouts: 16.1 us -> none  [local(): jnp.einsum('bhqk,bke->bqhe', p, v, preferred_element_type=jnp.float32)]
  transfers between devices with their start and end apart: 1 -> 0, of which waited for: 1 -> 0; matrix products, arithmetic and copies ran while one was open for 0% -> 0% of each run, Pallas kernels for 0% -> 0%
where the time goes in v1:
time: 458 us
  Pallas kernels  426 us (93%)
  local copies, waits for them, and re-layouts  31.7 us (7%)
    pallas_call x1, Pallas kernels, local(): pl.pallas_call(functools.partial(kernel, n_tp, s), out_shape=jax.ShapeDty...  426 us
    unnamed x1, local copies, waits for them, and re-layouts  29 us

profile of v1, /device:TPU:81, one launch (start us, length us, event | category | flops | bytes accessed | tf_op | source)
XLA Modules:
  0.0 457.6 jit_solution(7970681412622519419)
XLA Ops:
  0.0 1.3 reshape.13.gamma
  1.3 1.3 reshape.14.beta
  2.6 425.9 %shard_map.91 = bf16[6144,3584]{1,0:T(8,128)(2,1)} custom-call(bf16[6144,3584]{1,0:T(8,128)(2,1)} %bitcast.3, f32[1,3584]{1,0:T(1,128)} %reshape.13.gamma, f32[1,3584]{1,0:T(1,128)} %reshape.14.beta, bf16[3584,512]{1,0:T(8,128)(2,1)} %wq.1, bf16[3584,512]{1,0:T(8,128)(2,1)} %wkv.1, bf16[512,3584]{1,0:T(8,128)(2,1)} %wo.1, bf16[3584,1792]{1,0:T(8,128)(2,1)} %w1.1, ...), custom_call_target="tpu_custom_call" | custom-call | tf_op jit(solution)/shard_map/pallas_call | solution.py:327
  428.6 29.0 %copy.11 = bf16[4,1536,3584]{2,1,0:T(8,128)(2,1)} copy(bf16[4,1536,3584]{2,1,0:T(8,128)(2,1)} %bitcast.2) | data formatting | bytes 88080384

commit v2 on v1

v2 whole, which is shorter than its diff:
```python
import functools

import jax
import jax.numpy as jnp
from jax import lax
from jax.experimental import pallas as pl
from jax.experimental.pallas import tpu as pltpu
from jax.sharding import PartitionSpec as P

EPS = 1e-5
MESH = pl.DeviceIdType.MESH
TOK = 256
LOG2E = 1.4426950408889634
F32 = jnp.float32
BF16 = jnp.bfloat16
VMEM_LIMIT = 22 * 1024 * 1024


def kernel(n_tp, seq,
           x, gamma, beta, wq, wkv, wo, w1, w3, w2,
           y, wbuf,
           gb, wqkv, xin, lnst, ln, kv, act, part, pbuf, r1, r2, ybuf, xres,
           wsem, xsem, xrsem, lns, lnr, free, kvs, kvr, ds_, dr_, s1s, s1r, s2s, s2r, ts, tr,
           ys, yr, fs, fr, gs, gr, vsem):
    d = x.shape[1]
    n = x.shape[0] // TOK
    per_seq = seq // TOK
    dq = wq.shape[1]
    dh = wkv.shape[1] // 2
    ff = w1.shape[1]
    nh = dq // dh
    half = TOK // 2
    chips = n_tp // 2
    blk = half // chips
    dm = d // 2
    w13, w2o = wbuf.at[pl.ds(0, d)], wbuf.at[pl.ds(d, dq + ff)]

    me = lax.axis_index("tp")
    h = lax.rem(me, 2)
    c = me // 2
    cp = lax.rem(c + 1, chips)
    cm = lax.rem(c + chips - 1, chips)
    co = lax.rem(c + 2, chips)
    plus, minus, partner = cp * 2 + h, cm * 2 + h, c * 2 + 1 - h
    ca, cb = pl.ds(0, dm), pl.ds(dm, dm)

    def rcopy(src, dst, ssem, rsem, dev):
        return pltpu.make_async_remote_copy(src_ref=src, dst_ref=dst, send_sem=ssem, recv_sem=rsem,
                                            device_id={"tp": dev}, device_id_type=MESH)

    def own(ref):
        return ref.at[pl.ds(pl.multiple_of(h * half, half), half)]

    def rows_of(k):
        return pl.ds(pl.multiple_of(k * blk, blk), blk)

    def yrows(j, k):
        return pl.ds(pl.multiple_of(j * TOK + h * half + k * blk, blk), blk)

    def x_copy(j):
        return pltpu.make_async_copy(x.at[pl.ds(pl.multiple_of(j * TOK + h * half, half), half)], xin, xsem)

    def xres_copy(j):
        return pltpu.make_async_copy(x.at[yrows(j, c)], xres.at[lax.rem(j, 2)], xrsem.at[lax.rem(j, 2)])

    w_copies = (
        pltpu.make_async_copy(wq, wqkv.at[:, pl.ds(0, dq)], wsem.at[0]),
        pltpu.make_async_copy(wkv.at[:, pl.ds(pl.multiple_of(h * dh, dh), dh)], wqkv.at[:, pl.ds(dq, dh)], wsem.at[1]),
        pltpu.make_async_copy(w1, w13.at[:, pl.ds(0, ff)], wsem.at[2]),
        pltpu.make_async_copy(w3, w13.at[:, pl.ds(ff, ff)], wsem.at[3]),
        pltpu.make_async_copy(wo, w2o.at[pl.ds(0, dq)], wsem.at[4]),
        pltpu.make_async_copy(w2, w2o.at[pl.ds(dq, ff)], wsem.at[5]),
    )

    def layer_norm():
        for r in range(0, half, 16):
            xf = xin[r:r + 16, :].astype(F32)
            mu = jnp.mean(xf, axis=-1, keepdims=True)
            xc = xf - mu
            var = jnp.mean(jnp.square(xc), axis=-1, keepdims=True)
            lnst[r:r + 16, :] = (xc * lax.rsqrt(var + EPS) * gb[0:1, :] + gb[1:2, :]).astype(BF16)

    def ln_local():
        ln[pl.ds(pl.multiple_of(h * half, half), half), :] = lnst[...]

    def ln_copy():
        return rcopy(lnst, own(ln), lns, lnr, partner)

    def kv_copy(t):
        view = kv.at[h, pl.ds(pl.multiple_of(lax.rem(t, per_seq) * TOK, TOK), TOK)]
        return rcopy(view, view, kvs, kvr, partner)

    def d2d_copy(j, q):
        s = lax.rem(j, 2)
        cols = (ca, cb)[q]
        return rcopy(part.at[pl.ds(pl.multiple_of((1 - h) * half, half), half), cols], pbuf.at[s, :, cols],
                     ds_.at[s, q], dr_.at[s, q], partner)

    def s1_copies(j):
        s = lax.rem(j, 2)
        return (rcopy(pbuf.at[s, rows_of(co), ca], r1.at[s, 0], s1s.at[s, 0], s1r.at[s, 0], plus),
                rcopy(pbuf.at[s, rows_of(co), cb], r1.at[s, 1], s1s.at[s, 1], s1r.at[s, 1], minus))

    def t_copies(j):
        s = lax.rem(j, 2)
        return (rcopy(pbuf.at[s, rows_of(cp), cb], r2.at[s, 0, :, cb], ts.at[s, 0], tr.at[s, 0], plus),
                rcopy(pbuf.at[s, rows_of(cm), ca], r2.at[s, 1, :, ca], ts.at[s, 1], tr.at[s, 1], minus))

    def s2_copies(j):
        s = lax.rem(j, 2)
        return (rcopy(pbuf.at[s, rows_of(cp), ca], r2.at[s, 0, :, ca], s2s.at[s, 0], s2r.at[s, 0], plus),
                rcopy(pbuf.at[s, rows_of(cm), cb], r2.at[s, 1, :, cb], s2s.at[s, 1], s2r.at[s, 1], minus))

    def y_copies(j, k0, k1, k2):
        s = lax.rem(j, 2)
        parts = ((k0, ca, plus), (k1, cb, minus), (k0, cb, plus), (k1, ca, minus))
        out = [rcopy(ybuf.at[s, :, cols], y.at[yrows(j, k), cols], ys.at[s, i], yr.at[s, i], dev)
               for i, (k, cols, dev) in enumerate(parts)]
        return out + [rcopy(ybuf.at[s], y.at[yrows(j, k2)], ys.at[s, 4], yr.at[s, 4], partner)]

    def y_local(j):
        s = lax.rem(j, 2)
        return pltpu.make_async_copy(ybuf.at[s], y.at[yrows(j, c)], ys.at[s, 5])

    def f_copies(j):
        s = lax.rem(j, 2)
        va, vb = y.at[yrows(j, cm), ca], y.at[yrows(j, cp), cb]
        vm, vp = y.at[yrows(j, cm)], y.at[yrows(j, cp)]
        return (rcopy(va, va, fs.at[s, 0], fr.at[s, 0], plus),
                rcopy(vb, vb, fs.at[s, 1], fr.at[s, 1], minus),
                rcopy(vm, vm, fs.at[s, 2], fr.at[s, 2], partner),
                rcopy(vp, vp, fs.at[s, 3], fr.at[s, 3], partner))

    def g_copy(j):
        s3 = lax.rem(j, 3)
        v = y.at[yrows(j, co)]
        return rcopy(v, v, gs.at[s3], gr.at[s3], partner)

    def s1(j):
        s = lax.rem(j, 2)
        d2d_copy(j, 1).wait_recv()
        d2d_copy(j, 0).wait_send()
        d2d_copy(j, 1).wait_send()

        @pl.loop(0, half // 32)
        def _(i):
            a = part[pl.ds(pl.multiple_of(h * half + i * 32, 32), 32), :].astype(F32)
            rr = pl.ds(pl.multiple_of(i * 32, 32), 32)
            pbuf[s, rr, :] = (a + pbuf[s, rr, :].astype(F32)).astype(BF16)

        for cpy in s1_copies(j) + t_copies(j):
            cpy.start()
        xres_copy(j).start()

    def s2(j):
        s = lax.rem(j, 2)
        first = s1_copies(j)
        for cpy in first:
            cpy.wait_recv()
        pbuf[s, rows_of(cp), :dm] = (pbuf[s, rows_of(cp), :dm].astype(F32) + r1[s, 0].astype(F32)).astype(BF16)
        pbuf[s, rows_of(cm), dm:] = (pbuf[s, rows_of(cm), dm:].astype(F32) + r1[s, 1].astype(F32)).astype(BF16)
        for cpy in s2_copies(j):
            cpy.start()
        for cpy in first:
            cpy.wait_send()

    def s3(j):
        s = lax.rem(j, 2)
        copies = t_copies(j) + s2_copies(j)
        for cpy in copies:
            cpy.wait_recv()
        xres_copy(j).wait()
        ybuf[s] = (xres[s].astype(F32) + ((pbuf[s, rows_of(c), :].astype(F32) + r2[s, 0].astype(F32))
                                          + r2[s, 1].astype(F32))).astype(BF16)
        for cpy in y_copies(j, c, c, c):
            cpy.start()
        y_local(j).start()
        for cpy in copies:
            cpy.wait_send()

    def s4(j):
        came = y_copies(j, cm, cp, c)
        came[0].wait_recv()
        came[1].wait_recv()
        onward = f_copies(j)
        onward[0].start()
        onward[1].start()
        for cpy in came[2:]:
            cpy.wait_recv()
        onward[2].start()
        onward[3].start()
        for cpy in y_copies(j, c, c, c):
            cpy.wait_send()
        y_local(j).wait()

    def s5(j):
        for cpy in f_copies(j):
            cpy.wait_recv()
        g_copy(j).start()
        for cpy in f_copies(j):
            cpy.wait_send()

    def s6(j):
        g_copy(j).wait_recv()
        g_copy(j).wait_send()

    def hidden(j0, j1):
        lhs = ln[...]
        tile = min(256, ff)
        for j in range(j0 * tile, j1 * tile, tile):
            g = jnp.dot(lhs, w13[:, j:j + tile], preferred_element_type=F32)
            u = jnp.dot(lhs, w13[:, ff + j:ff + j + tile], preferred_element_type=F32)
            act[:, dq + j:dq + j + tile] = (jax.nn.silu(g) * u).astype(BF16)

    tiles = ff // min(256, ff)
    first_tiles = min(3, tiles - 1)

    def attend(t, blocks):
        keys = blocks * TOK
        k = kv[0, :keys, :]
        v = kv[1, :keys, :]
        open_ = max(keys - 2 * TOK, 0)
        qi = lax.broadcasted_iota(jnp.int32, (TOK, keys - open_), 0)
        ki = lax.broadcasted_iota(jnp.int32, (TOK, keys - open_), 1)
        seen = ki + open_ <= qi + lax.rem(t, per_seq) * TOK
        rest = list(range(first_tiles, tiles))
        for a in range(nh):
            q = act[:, a * dh:(a + 1) * dh]
            sc = lax.dot_general(q, k, (((1,), (1,)), ((), ())), preferred_element_type=F32)
            sc = sc * (dh ** -0.5 * LOG2E)
            if rest:
                j = rest.pop(0)
                hidden(j, j + 1)
            last = jnp.where(seen, sc[:, open_:], -1e30)
            sc = last if open_ == 0 else jnp.concatenate([sc[:, :open_], last], axis=1)
            p = jnp.exp2(sc - jnp.max(sc, axis=-1, keepdims=True))
            p = (p * (1.0 / jnp.sum(p, axis=-1, keepdims=True))).astype(BF16)
            if rest and a + 1 < nh:
                j = rest.pop(0)
                hidden(j, j + 1)
            act[:, a * dh:(a + 1) * dh] = jnp.dot(p, v, preferred_element_type=F32).astype(BF16)
        for j in rest:
            hidden(j, j + 1)

    in13, in_vmem = vmem_steps(n, d, dq, ff)
    early = max(min(in_vmem, n - 4), in13)

    def v_copy(j, steps, i):
        rows = pl.ds(j * TOK, steps * TOK)
        return pltpu.make_async_copy(y.at[rows], wbuf.at[rows], vsem.at[i])

    barrier = pltpu.get_barrier_semaphore()
    for dev in (partner, plus, minus):
        pl.semaphore_signal(barrier, inc=1, device_id={"tp": dev}, device_id_type=MESH)
    x_copy(0).start()
    for cpy in w_copies:
        cpy.start()
    gb[0:1, :] = gamma[...][None, :]
    gb[1:2, :] = beta[...][None, :]
    pl.semaphore_wait(barrier, 3)
    x_copy(0).wait()
    layer_norm()
    ln_local()
    x_copy(1).start()
    ln_copy().start()

    @pl.loop(0, n + 4)
    def _(t):
        @pl.when((t >= 1) & (t <= n))
        def _():
            d2d_copy(t - 1, 0).wait_recv()

        @pl.when(t < n)
        def _():
            ln_copy().wait_recv()
            ln_copy().wait_send()

            @pl.when(t == 0)
            def _():
                for cpy in w_copies[:4]:
                    cpy.wait()

            @pl.when(t + 1 < n)
            def _():
                x_copy(t + 1).wait()

            layer_norm()
            pos = lax.rem(t, per_seq)
            here = pl.ds(pl.multiple_of(pos * TOK, TOK), TOK)
            after = jnp.where(lax.rem(pos, 2) == 0, pos + 1, per_seq)
            kv[1, pl.ds(pl.multiple_of(after * TOK, TOK), TOK), :] = jnp.zeros((TOK, dh), BF16)
            qkv = jnp.dot(ln[...], wqkv[...], preferred_element_type=F32).astype(BF16)
            act[:, :dq] = qkv[:, :dq]
            kv[h, here, :] = qkv[:, dq:]
            kv_copy(t).start()
            hidden(0, first_tiles)

            @pl.when(t + 2 < n)
            def _():
                x_copy(t + 2).start()

        @pl.when((t >= 1) & (t <= n))
        def _():
            s1(t - 1)

        @pl.when(t < n)
        def _():
            kv_copy(t).wait_recv()
            kv_copy(t).wait_send()
            for b in range(0, per_seq, 2):
                pos = lax.rem(t, per_seq)
                pl.when((pos == b) | (pos == b + 1))(functools.partial(attend, t, b + 2))
            pl.semaphore_signal(free, inc=1, device_id={"tp": partner}, device_id_type=MESH)

            @pl.when(t + 1 < n)
            def _():
                ln_local()

            @pl.when(t == n - 1)
            def _():
                v_copy(0, in13, 0).start()

        @pl.when((t >= 1) & (t <= n))
        def _():
            s2(t - 1)

        @pl.when((t >= 2) & (t <= n + 1))
        def _():
            s4(t - 2)

        @pl.when(t < n)
        def _():
            pl.semaphore_wait(free, 1)

            @pl.when(t + 1 < n)
            def _():
                ln_copy().start()

            @pl.when(t == 0)
            def _():
                for cpy in w_copies[4:]:
                    cpy.wait()

            lhs = act[...]
            tile = min(256, dm)
            for q in range(2):
                for j in range(q * dm, (q + 1) * dm, tile):
                    part[:, j:j + tile] = jnp.dot(lhs, w2o[:, j:j + tile], preferred_element_type=F32).astype(BF16)
                d2d_copy(t, q).start()

        @pl.when((t >= 3) & (t <= n + 2))
        def _():
            s5(t - 3)

        @pl.when((t >= 1) & (t <= n))
        def _():
            s3(t - 1)

        @pl.when(t >= 4)
        def _():
            s6(t - 4)

        if early > in13:
            @pl.when(t == n - 1)
            def _():
                v_copy(in13, early - in13, 1).start()

        for i, j in enumerate(range(early, in_vmem)):
            @pl.when(t == j + 4)
            def _():
                v_copy(j, 1, 2 + i).start()

    v_copy(0, in13, 0).wait()
    if early > in13:
        v_copy(in13, early - in13, 1).wait()
    for i, j in enumerate(range(early, in_vmem)):
        v_copy(j, 1, 2 + i).wait()


def vmem_steps(n, d, dq, ff):
    in13 = d // TOK
    return in13, min(in13 + (dq + ff) // TOK, n - 1)


def finish(n, in_vmem, y, wbuf, out, buf, sem):
    loads = [pltpu.make_async_copy(y.at[pl.ds(j * TOK, TOK)], buf.at[j - in_vmem], sem.at[j]) for j in range(in_vmem, n)]
    stores = [pltpu.make_async_copy(wbuf.at[pl.ds(j * TOK, TOK)] if j < in_vmem else buf.at[j - in_vmem],
                                    out.at[pl.ds(j * TOK, TOK)], sem.at[n + j]) for j in range(n)]
    for cpy in loads + stores[:in_vmem]:
        cpy.start()
    for load, store in zip(loads, stores[in_vmem:]):
        load.wait()
        store.start()
    for cpy in stores:
        cpy.wait()


def solution(mesh):
    n_tp = mesh.shape["tp"]

    def local(x, gamma, beta, wq, wkv, wo, w1, w3, w2):
        b, s, d = x.shape
        dq, dh, ff = wq.shape[1], wkv.shape[1] // 2, w1.shape[1]
        n = b * s // TOK
        half = TOK // 2
        blk = half // (n_tp // 2)
        in13, in_vmem = vmem_steps(n, d, dq, ff)
        assert 2 * ff == d and in13 <= n - 5 and n_tp == 8
        dma = pltpu.SemaphoreType.DMA
        hbm = pl.BlockSpec(memory_space=pl.ANY)
        vmem = pl.BlockSpec(memory_space=pltpu.VMEM)
        y, wbuf = pl.pallas_call(
            functools.partial(kernel, n_tp, s),
            out_shape=(jax.ShapeDtypeStruct((b * s, d), BF16), pltpu.VMEM((d + dq + ff, d), BF16)),
            in_specs=[hbm, vmem, vmem] + [hbm] * 6,
            out_specs=(hbm, vmem),
            scratch_shapes=[
                pltpu.VMEM((2, d), F32),
                pltpu.VMEM((d, dq + dh), BF16),
                pltpu.VMEM((half, d), BF16),
                pltpu.VMEM((half, d), BF16),
                pltpu.VMEM((TOK, d), BF16),
                pltpu.VMEM((2, s + TOK, dh), BF16),
                pltpu.VMEM((TOK, dq + ff), BF16),
                pltpu.VMEM((TOK, d), BF16),
                pltpu.VMEM((2, half, d), BF16),
                pltpu.VMEM((2, 2, blk, d // 2), BF16),
                pltpu.VMEM((2, 2, blk, d), BF16),
                pltpu.VMEM((2, blk, d), BF16),
                pltpu.VMEM((2, blk, d), BF16),
                dma((6,)), dma, dma((2,)), dma, dma, pltpu.SemaphoreType.REGULAR, dma, dma,
                dma((2, 2)), dma((2, 2)), dma((2, 2)), dma((2, 2)), dma((2, 2)), dma((2, 2)), dma((2, 2)), dma((2, 2)),
                dma((2, 6)), dma((2, 5)), dma((2, 4)), dma((2, 4)), dma((3,)), dma((3,)), dma((6,)),
            ],
            compiler_params=pltpu.CompilerParams(collective_id=0, has_side_effects=True,
                                                 vmem_limit_bytes=VMEM_LIMIT),
        )(x.reshape(b * s, d), gamma, beta, wq, wkv, wo, w1, w3, w2)
        out = pl.pallas_call(
            functools.partial(finish, n, in_vmem),
            out_shape=jax.ShapeDtypeStruct((b * s, d), BF16),
            in_specs=[hbm, vmem],
            out_specs=hbm,
            scratch_shapes=[pltpu.VMEM((n - in_vmem, TOK, d), BF16), dma((2 * n,))],
            compiler_params=pltpu.CompilerParams(vmem_limit_bytes=8 * 1024 * 1024),
        )(y, wbuf)
        return out.reshape(b, s, d)

    return jax.shard_map(local, mesh=mesh,
                         in_specs=(P('dp', None, None), P(), P(), P(None, 'tp'), P(), P('tp', None),
                                   P(None, 'tp'), P(None, 'tp'), P('tp', None)),
                         out_specs=P('dp', None, None), check_vma=False)
```

time: 458 us -> 455 us (level)
  local copies, waits for them, and re-layouts: 31.7 us -> 0 us
  Pallas kernels: 426 us -> 455 us
    unnamed x1 -> x0, local copies, waits for them, and re-layouts: 29 us -> none
    pallas_call x1 -> x2, Pallas kernels: 426 us -> 455 us  [the longest x1 440 us: local(): pl.pallas_call(functools.partial(kernel, n_tp, s), out_shape=(jax.ShapeDt...]
where the time goes in v2:
time: 455 us
  Pallas kernels  455 us (100%)
    pallas_call x1, Pallas kernels, local(): pl.pallas_call(functools.partial(kernel, n_tp, s), out_shape=(jax.ShapeDt...  440 us
    pallas_call x1, Pallas kernels, local(): pl.pallas_call(functools.partial(finish, n, in_vmem), out_shape=jax.Shape...  14.5 us

profile of v2, /device:TPU:81, one launch (start us, length us, event | category | flops | bytes accessed | tf_op | source)
XLA Modules:
  0.0 454.8 jit_solution(16398698377104912255)
XLA Ops:
  0.0 440.3 %shard_map.91 = (bf16[6144,3584]{1,0:T(8,128)(2,1)}, bf16[5888,3584]{1,0:T(8,128)(2,1)S(1)}) custom-call(bf16[6144,3584]{1,0:T(8,128)(2,1)} %bitcast.2, f32[3584]{0:T(1024)} %gamma.1, f32[3584]{0:T(1024)} %beta.1, bf16[3584,512]{1,0:T(8,128)(2,1)} %wq.1, bf16[3584,512]{1,0:T(8,128)(2,1)} %wkv.1, bf16[512,3584]{1,0:T(8,128)(2,1)} %wo.1, ...), custom_call_target="tpu_custom_call" | custom-call | tf_op jit(solution)/shard_map/pallas_call | solution.py:412
  440.3 14.5 %shard_map.92 = bf16[6144,3584]{1,0:T(8,128)(2,1)} custom-call(bf16[6144,3584]{1,0:T(8,128)(2,1)} %get-tuple-element.7.y, bf16[5888,3584]{1,0:T(8,128)(2,1)S(1)} %get-tuple-element.8.wbuf), custom_call_target="tpu_custom_call" | custom-call | tf_op jit(solution)/shard_map/pallas_call | solution.py:438
